TPU v7x, 32 devices: a whole 2x2x4 slice. The times are simulated.
32 devices in a mesh: dp: 8 (over z, y), sp: 4 (over x, core).
Axes of the slice: x: 2, y: 2, z: 4, core: 2. Of those that a mesh axis runs over, the one named last changes fastest.
Arguments:
- latents: bfloat16 [24, 48, 96, 384], P('dp', 'sp')
- t_mod: float32 [24, 6, 384], P('dp')
- t_mod_zero: float32 [24, 6, 384], P('dp')
- frame_mask: int32 [24, 48], P('dp')
- captions: bfloat16 [24, 120, 384], P('dp')
- caption_len: int32 [24], P('dp')
- w_qkv: bfloat16 [2, 384, 3, 6, 64], replicated
- w_out: bfloat16 [2, 6, 64, 384], replicated
- w_cross_q: bfloat16 [2, 384, 6, 64], replicated
- w_cross_kv: bfloat16 [2, 384, 2, 6, 64], replicated
- w_cross_out: bfloat16 [2, 6, 64, 384], replicated
- w_mlp_in: bfloat16 [2, 384, 1536], replicated
- w_mlp_out: bfloat16 [2, 1536, 384], replicated
- mod_table: float32 [2, 6, 384], replicated
- grad_out: bfloat16 [24, 48, 96, 384], P('dp', 'sp')
Outputs:
- output 1: bfloat16 [24, 48, 96, 384], P('dp', 'sp')
- output 2: float32 [2, 384, 3, 6, 64], replicated
- output 3: float32 [2, 6, 64, 384], replicated
- output 4: float32 [2, 384, 6, 64], replicated
- output 5: float32 [2, 384, 2, 6, 64], replicated
- output 6: float32 [2, 6, 64, 384], replicated
- output 7: float32 [2, 384, 1536], replicated
- output 8: float32 [2, 1536, 384], replicated
- output 9: float32 [2, 6, 384], replicated
All inputs are finite; a program needn't handle non-finite values.
Results may differ from a plain program's by a relative error of at most 0.02.
Values are sent between devices in bfloat16 or wider.
A program may use at most 1 GiB of HBM per device.

v0:
```python
import jax
import jax.numpy as jnp
from jax import lax
from jax.sharding import PartitionSpec as P, NamedSharding


def layer_norm(hidden_in):
    centered = hidden_in - jnp.mean(hidden_in, axis=-1, keepdims=True)
    return centered * lax.rsqrt(jnp.mean(jnp.square(centered), axis=-1, keepdims=True) + 1e-6)


def rms_heads(head_vec):
    return head_vec * lax.rsqrt(jnp.mean(jnp.square(head_vec), axis=-1, keepdims=True) + 1e-6)


def rotary(head_vec):
    half = head_vec.shape[-1] // 2
    inv_freq = 10000.0 ** (-jnp.arange(half, dtype=jnp.float32) / half)
    angle = jnp.arange(head_vec.shape[1], dtype=jnp.float32)[:, None] * inv_freq[None, :]
    cosine = jnp.cos(angle)[None, :, None, None, :]
    sine = jnp.sin(angle)[None, :, None, None, :]
    first = head_vec[..., :half]
    second = head_vec[..., half:]
    return jnp.concatenate([first * cosine - second * sine, first * sine + second * cosine], axis=-1)


def modulation(mod_table, base):
    mod_terms = (mod_table + base)[:, :, None]
    return [mod_terms[:, :, :, index] for index in range(6)]


def attn_inputs(w_qkv, latents, shift_att, scale_att, temporal):
    normed = (layer_norm(latents.astype(jnp.float32)) * (1.0 + scale_att) + shift_att).astype(jnp.bfloat16)
    qkv_all = jnp.einsum('btsd,dkhe->btskhe', normed, w_qkv, preferred_element_type=jnp.float32)
    query = rms_heads(qkv_all[:, :, :, 0])
    keys = rms_heads(qkv_all[:, :, :, 1])
    if temporal:
        query = rotary(query)
        keys = rotary(keys)
    return query.astype(jnp.bfloat16), keys.astype(jnp.bfloat16), qkv_all[:, :, :, 2].astype(jnp.bfloat16)


def attn_core(query, keys, values, temporal):
    attn_scale = query.shape[-1] ** -0.5
    if temporal:
        scores = jnp.einsum('bqshe,bkshe->bshqk', query, keys, preferred_element_type=jnp.float32)
        attn_prob = jax.nn.softmax(scores * attn_scale, axis=-1).astype(jnp.bfloat16)
        heads_out = jnp.einsum('bshqk,bkshe->bqshe', attn_prob, values, preferred_element_type=jnp.float32)
    else:
        scores = jnp.einsum('btqhe,btkhe->bthqk', query, keys, preferred_element_type=jnp.float32)
        attn_prob = jax.nn.softmax(scores * attn_scale, axis=-1).astype(jnp.bfloat16)
        heads_out = jnp.einsum('bthqk,btkhe->btqhe', attn_prob, values, preferred_element_type=jnp.float32)
    return heads_out.astype(jnp.bfloat16)


def block_rest(weight_set, latents, heads_out, mod_terms, captions, caption_len):
    w_out, w_cross_q, w_cross_kv, w_cross_out, w_mlp_in, w_mlp_out = weight_set
    gate_att = mod_terms[2]
    shift_mlp = mod_terms[3]
    scale_mlp = mod_terms[4]
    gate_mlp = mod_terms[5]
    attn_scale = w_cross_q.shape[-1] ** -0.5
    attn_proj = jnp.einsum('btshe,hed->btsd', heads_out, w_out, preferred_element_type=jnp.float32)
    residual = (latents.astype(jnp.float32) + gate_att * attn_proj).astype(jnp.bfloat16)
    batch = residual.shape[0]
    tokens = residual.shape[1] * residual.shape[2]
    cross_q = jnp.einsum('btsd,dhe->btshe', residual, w_cross_q, preferred_element_type=jnp.float32).astype(jnp.bfloat16)
    cross_q = cross_q.reshape(batch, tokens, w_cross_q.shape[1], w_cross_q.shape[2])
    cross_kv = jnp.einsum('bmd,dkhe->bmkhe', captions, w_cross_kv, preferred_element_type=jnp.float32).astype(jnp.bfloat16)
    scores = jnp.einsum('bnhe,bmhe->bhnm', cross_q, cross_kv[:, :, 0], preferred_element_type=jnp.float32) * attn_scale
    key_valid = jnp.arange(captions.shape[1])[None, None, None, :] < caption_len[:, None, None, None]
    attn_prob = jax.nn.softmax(jnp.where(key_valid, scores, -1e30), axis=-1).astype(jnp.bfloat16)
    cross_heads = jnp.einsum('bhnm,bmhe->bnhe', attn_prob, cross_kv[:, :, 1], preferred_element_type=jnp.float32).astype(jnp.bfloat16)
    cross_proj = jnp.einsum('bnhe,hed->bnd', cross_heads, w_cross_out, preferred_element_type=jnp.float32)
    residual = (residual.astype(jnp.float32) + cross_proj.reshape(residual.shape)).astype(jnp.bfloat16).astype(jnp.float32)
    normed = (layer_norm(residual) * (1.0 + scale_mlp) + shift_mlp).astype(jnp.bfloat16)
    hidden = jax.nn.gelu(jnp.dot(normed, w_mlp_in, preferred_element_type=jnp.float32), approximate=True).astype(jnp.bfloat16)
    mlp_out = jnp.dot(hidden, w_mlp_out, preferred_element_type=jnp.float32)
    return (residual + gate_mlp * mlp_out).astype(jnp.bfloat16)


def block_forward(weight_set, latents, base, captions, caption_len, temporal):
    mod_terms = modulation(weight_set[7], base)
    query, keys, values = attn_inputs(weight_set[0], latents, mod_terms[0], mod_terms[1], temporal)
    heads_out = attn_core(query, keys, values, temporal)
    return block_rest(weight_set[1:7], latents, heads_out, mod_terms, captions, caption_len)


def solution(mesh):
    tok_spec = P('dp', 'sp')
    row_spec = P('dp')
    in_specs = (tok_spec, row_spec, row_spec, row_spec, row_spec, row_spec, P(), P(), P(), P(), P(), P(), P(), P(), tok_spec)
    out_specs = (tok_spec, P(), P(), P(), P(), P(), P(), P(), P())

    def local_step(latents, t_mod, t_mod_zero, frame_mask, captions, caption_len, w_qkv, w_out, w_cross_q, w_cross_kv, w_cross_out, w_mlp_in, w_mlp_out, mod_table, grad_out):
        param_set = (w_qkv, w_out, w_cross_q, w_cross_kv, w_cross_out, w_mlp_in, w_mlp_out, mod_table)
        first = tuple(param[0] for param in param_set)
        second = tuple(param[1] for param in param_set)
        base_all = jnp.where(frame_mask[:, :, None, None] == 1, t_mod[:, None], t_mod_zero[:, None])
        local_frames = latents.shape[1]
        base_local = lax.dynamic_slice_in_dim(base_all, lax.axis_index('sp') * local_frames, local_frames, axis=1)

        def spatial(weight_set, lat_in):
            return block_forward(weight_set, lat_in, base_local, captions, caption_len, False)

        def temporal(weight_set, lat_in):
            return block_forward(weight_set, lat_in, base_all, captions, caption_len, True)

        middle, spatial_pull = jax.vjp(spatial, first, latents)
        middle_cols = lax.all_to_all(middle, 'sp', 2, 1, tiled=True)
        fwd_out, temporal_pull = jax.vjp(temporal, second, middle_cols)
        grad_cols = lax.all_to_all(grad_out, 'sp', 2, 1, tiled=True)
        grads_second, grad_mid_cols = temporal_pull(grad_cols)
        grad_mid = lax.all_to_all(grad_mid_cols, 'sp', 1, 2, tiled=True)
        grads_first, grad_latents = spatial_pull(grad_mid)
        grads = tuple(jnp.stack([grad_a.astype(jnp.float32), grad_b.astype(jnp.float32)]) for grad_a, grad_b in zip(grads_first, grads_second))
        grads = lax.psum(grads, ('dp', 'sp'))
        return (grad_latents,) + grads

    return jax.shard_map(local_step, mesh=mesh, in_specs=in_specs, out_specs=out_specs, check_vma=False)
```

profile of v0, /device:TPU:0, one launch (start us, length us, event | category | flops | bytes accessed | tf_op | source)
XLA Modules:
  0.0 1232.5 jit_solution(3169194445689867778)
XLA Ops:
  33.6 11.1 fusion.443
  104.0 12.0 multiply_convert_fusion.1
  147.0 25.9 %all-to-all-done.1 = bf16[3,12,96,384]{3,1,0,2:T(8,128)(2,1)} async-done(((bf16[3,12,96,384]{3,1,0,2:T(8,128)(2,1)}), bf16[3,12,96,384]{3,1,0,2:T(8,128)(2,1)}, u32[]{:S(2)}, u32[]{:S(2)}) %all-to-all-start.1) | async-done | bytes 2654240 | tf_op jit(solution)/shard_map/all_to_all | solution.py:110
  186.1 13.1 %fusion.365 = f32[3,48,24,3,6,64]{5,2,4,3,1,0:T(8,128)} fusion(bf16[3,48,24,384,1,1]{3,2,5,4,1,0:T(8,128)(2,1)S(1)} %bitcast.813, bf16[2,384,3,6,64]{1,4,3,2,0:T(8,128)(2,1)S(1)} %copy-done.113), kind=kOutput, calls=%fused_computation.416 | convolution fusion | flops 3057647616 | bytes 19464192 | tf_op jit(solution)/shard_map/jvp(btsd,dkhe->btskhe)/dot_general | solution.py:34
  199.3 10.0 multiply_reduce_fusion.3
  219.7 20.5 %fusion.52 = (f32[3,48,24,6,64]{4,2,3,1,0:T(8,128)}, f32[3,48,24,6,64]{4,2,3,1,0:T(8,128)}) fusion(f32[3,48,24,3,6,64]{5,2,4,3,1,0:T(8,128)} %fusion.365, f32[3,48,24,6]{2,3,1,0:T(8,128)S(1)} %fusion.382, f32[3,48,24,6]{2,3,1,0:T(8,128)S(1)} %fusion.383), kind=kLoop, calls=%fused_computation.110 | loop fusion | flops 2654208 | bytes 21399552 | tf_op jit(solution)/shard_map/jvp()/mul | solution.py:13
  240.3 24.0 %subtract_convert_fusion.1 = (bf16[3,48,24,6,32]{4,2,3,1,0:T(8,128)(2,1)}, bf16[3,48,24,6,32]{4,2,3,1,0:T(8,128)(2,1)}, bf16[3,48,24,6,32]{4,2,3,1,0:T(8,128)(2,1)}, bf16[3,48,24,6,32]{4,2,3,1,0:T(8,128)(2,1)}) fusion(f32[3,48,24,6,64]{4,2,3,1,0:T(8,128)} %get-tuple-element.89, f32[48,32]{1,0:T(8,128)S(1)} %get-tuple-element.133, ...), kind=kLoop, calls=%fused_computation.82 | loop fusion | flops 10616832 | bytes 15937536 | tf_op jit(solution)/shard_map/convert.51
  290.9 14.2 %fusion.445 = (f32[3,24,6,48]{3,2,1,0:T(8,128)S(1)}, f32[3,24,6,48,48]{3,4,2,1,0:T(8,128)}) fusion(f32[3,24,6,48,48]{3,4,2,1,0:T(8,128)} %fusion.152), kind=kOutput, calls=%fused_computation.545 | output fusion | flops 3981359 | bytes 8045568 | tf_op jit(solution)/shard_map/jvp()/sub | solution.py:47
  305.1 10.9 convert_bitcast_fusion.4
  334.5 10.1 fusion.446
  369.9 10.7 fusion.318
  380.6 23.7 %fusion.7 = bf16[3,48,24,1536]{3,2,1,0:T(8,128)(2,1)} fusion(f32[3,48,24,1536]{3,2,1,0:T(8,128)} %fusion.318, bf16[3,48,24,384]{3,2,1,0:T(8,128)(2,1)S(1)} %bitcast.832, bf16[2,1536,384]{2,1,0:T(8,128)(2,1)S(1)} %copy-done.164), kind=kOutput, calls=%fused_computation.16 | convolution fusion | flops 4188340224 | bytes 35684352 | tf_op jit(solution)/shard_map/transpose(jvp())/dot_general | solution.py:78
  439.6 10.7 fusion.327
  483.5 16.6 %fusion.30 = (f32[3,24,6,48]{3,2,1,0:T(8,128)S(1)}, bf16[3,24,6,48,48]{3,4,2,1,0:T(8,128)(2,1)}) fusion(f32[3,24,6,48,48]{3,4,2,1,0:T(8,128)} %get-tuple-element.147, f32[3,24,6,48]{3,2,1,0:T(8,128)S(1)} %copy-done.52, bf16[3,48,24,6,64]{4,2,3,1,0:T(8,128)(2,1)} %fusion.119, bf16[3,24,6,64,48]{3,1,2,4,0:T(8,128)(2,1)} %convert_bitcast_fusion.3), kind=kOutput, calls=%fused_computation.52 | convolution fusion | flops 132357888 | bytes 11446272 | tf_op jit(solution)/shard_map/transpose(jvp(bshqk,bkshe->bqshe))/dot_general | solution.py:48
  500.2 11.4 fusion.150
  520.4 10.9 fusion.145
  532.5 14.7 %fusion.234 = bf16[1,1536,384]{2,1,0:T(8,128)(2,1)} fusion(f32[3,48,24,384]{3,2,1,0:T(8,128)} %bitcast.803, f32[3,48,384]{2,1,0:T(8,128)S(1)} %copy-done.147, f32[3,48,24,1536]{3,2,1,0:T(8,128)} %fusion.318), kind=kOutput, calls=%fused_computation.341 | convolution fusion | flops 4126556160 | bytes 27942912 | tf_op jit(solution)/shard_map/transpose(jvp())/dot_general | solution.py:78
  563.0 30.2 %multiply_add_fusion.1 = (f32[3,48,24,6,32]{4,2,3,1,0:T(8,128)}, f32[3,48,24,6,32]{4,2,3,1,0:T(8,128)}, f32[3,48,24,6,32]{4,2,3,1,0:T(8,128)}, f32[3,48,24,6,32]{4,2,3,1,0:T(8,128)}) fusion(f32[3,48,24,6,64]{4,2,3,1,0:T(8,128)} %convert_bitcast_fusion, f32[48,32]{1,0:T(8,128)S(1)} %copy-done.141, f32[48,32]{1,0:T(8,128)S(1)} %copy-done.139, ...), kind=kLoop, calls=%fused_computation.70 | loop fusion | flops 9289728 | bytes 21245952 | tf_op jit(solution)/shard_map/transpose(jvp())/add_any | solution.py:24
  593.2 24.4 %multiply_reduce_fusion.1 = (f32[3,48,24,6]{2,3,1,0:T(8,128)}, f32[3,48,24,6]{2,3,1,0:T(8,128)S(1)}) fusion(f32[3,48,24,3,6,64]{5,2,4,3,1,0:T(8,128)} %fusion.365, f32[3,48,24,6,32]{4,2,3,1,0:T(8,128)} %get-tuple-element.126, f32[3,48,24,6,32]{4,2,3,1,0:T(8,128)} %get-tuple-element.127, f32[3,48,24,6,32]{4,2,3,1,0:T(8,128)} %get-tuple-element.96, ...), kind=kLoop, calls=%fused_computation.72 | loop fusion | flops 7921152 | bytes 21399552 | tf_op jit(solution)/shard_map/transpose(jvp())/reduce_sum | solution.py:13
  619.4 28.2 %add_bitcast_fusion.1 = (f32[3,48,24,1,6,64]{5,2,4,1,0,3:T(8,128)}, f32[3,48,24,1,6,64]{5,2,4,1,0,3:T(8,128)}) fusion(f32[3,48,24,3,6,64]{5,2,4,3,1,0:T(8,128)} %fusion.365, f32[3,48,24,6]{2,3,1,0:T(8,128)S(1)} %multiply_multiply_fusion.5, f32[3,48,24,6]{2,3,1,0:T(8,128)S(1)} %copy-done.34, f32[3,48,24,6,32]{4,2,3,1,0:T(8,128)} %get-tuple-element.126, ...), kind=kLoop, calls=%fused_computation.71 | loop fusion | flops 10616832 | bytes 32182272 | tf_op jit(solution)/shard_map/transpose(jvp())/broadcast_in_dim | solution.py:36
  647.7 12.2 fusion.4
  685.8 14.0 %fusion.258 = bf16[1,384,3,6,64]{1,4,3,2,0:T(8,128)(2,1)} fusion(f32[3,48,24,384]{3,2,1,0:T(8,128)} %bitcast.774, f32[3,48,384]{2,1,0:T(8,128)S(1)} %copy-done.146, f32[3,48,24]{2,1,0:T(8,128)S(1)} %copy-done.61, f32[3,48,24]{2,1,0:T(8,128)S(1)} %get-tuple-element.123, f32[3,48,384]{2,1,0:T(8,128)S(1)} %copy-done.35, ...), kind=kOutput, calls=%fused_computation.360 | convolution fusion | flops 3076669440 | bytes 19934208 | tf_op jit(solution)/shard_map/transpose(jvp(btsd,dkhe->btskhe))/dot_general | solution.py:34
  699.8 10.6 all-to-all-done.2
  712.1 18.2 %fusion.11 = bf16[3,12,96,1536]{3,2,1,0:T(8,128)(2,1)S(1)} fusion(f32[3,12,96,1536]{3,2,1,0:T(8,128)} %get-tuple-element.143, bf16[3,12,96,384]{3,2,1,0:T(8,128)(2,1)S(1)} %bitcast.831, bf16[2,1536,384]{2,1,0:T(8,128)(2,1)S(1)} %copy-done.165), kind=kOutput, calls=%fused_computation.20 | convolution fusion | flops 4188340224 | bytes 35684352 | tf_op jit(solution)/shard_map/transpose(jvp())/dot_general | solution.py:78
  804.3 11.3 fusion.232
  825.3 12.2 fusion.35
  848.1 17.1 %fusion.67 = (f32[3,12,96,6]{2,3,1,0:T(8,128)}, f32[3,12,96,6]{2,3,1,0:T(8,128)S(1)}, bf16[3,12,6,96,64]{3,4,2,1,0:T(8,128)(2,1)}) fusion(f32[3,12,96,3,6,64]{2,5,4,3,1,0:T(8,128)} %copy-done.1, bf16[3,12,6,96,64]{3,4,2,1,0:T(8,128)(2,1)} %convolution_convert_fusion.11, bf16[3,12,96,6,64]{2,4,3,1,0:T(8,128)(2,1)} %get-tuple-element.94, ...), kind=kOutput, calls=%fused_computation.150 | convolution fusion | flops 274005504 | bytes 30855168 | tf_op jit(solution)/shard_map/transpose(jvp(btqhe,btkhe->bthqk))/dot_general | solution.py:50
  877.1 10.7 fusion.66
  887.8 12.3 fusion.263
  903.4 15.3 %multiply_reduce_fusion.8 = f32[3,48,384]{2,1,0:T(8,128)S(1)} fusion(f32[3,48,24,384]{3,2,1,0:T(8,128)} %bitcast.804, bf16[2,1536,384]{2,1,0:T(8,128)(2,1)} %param.27, f32[3,48,24,1536]{3,2,1,0:T(8,128)} %fusion.318), kind=kOutput, calls=%fused_computation.234 | convolution fusion | flops 4127238144 | bytes 27942912 | tf_op jit(solution)/shard_map/jvp()/dot_general | solution.py:78
  934.7 41.4 %psum.63 = f32[2,6,384]{2,1,0:T(8,128)S(1)} all-reduce(f32[2,6,384]{2,1,0:T(8,128)S(1)} %pad_maximum_fusion.2), channel_id=1, replica_groups=mesh['dp'=8,'sp'=4] {'dp','sp'}, use_global_device_ids=true, to_apply=%region_57.58 | all-reduce | flops 4608 | bytes 36864 | tf_op jit(solution)/shard_map/psum | solution.py:117
  982.3 228.4 %all-reduce.29.cloned.1.call-done = (f32[2,384,3,6,64]{1,4,3,2,0:T(8,128)}, f32[2,6,64,384]{3,2,1,0:T(8,128)}, f32[2,384,6,64]{1,3,2,0:T(8,128)}, f32[2,384,2,6,...) async-done(((f32[2,384,3,6,64]{1,4,3,2,0:T(8,128)}, f32[2,6,64,384]{3,2,1,0:T(8,128)}, ...) | async-done | bytes 18874384 | tf_op jit(solution)/shard_map/psum | solution.py:117
  (600 shorter events, 478.5 us)
Async XLA Ops:
  7.2 65.8 %copy-start = (bf16[3,120,384]{2,1,0:T(8,128)(2,1)S(1)}, bf16[3,120,384]{2,1,0:T(8,128)(2,1)}, u32[]{:S(2)}) copy-start(bf16[3,120,384]{2,1,0:T(8,128)(2,1)} %param.19) | copy-start | bytes 829444
  8.1 67.0 %copy-start.166 = (pred[3,120]{1,0:T(4,128)(4,1)}, pred[3,120]{1,0:T(4,128)(4,1)S(1)}, u32[]{:S(2)}) copy-start(pred[3,120]{1,0:T(4,128)(4,1)S(1)} %iota_compare_fusion) | copy-start | bytes 1084
  16.5 36.0 %copy-start.122 = (f32[3,12,384]{2,1,0:T(8,128)}, f32[3,12,384]{2,1,0:T(8,128)S(1)}, u32[]{:S(2)}) copy-start(f32[3,12,384]{2,1,0:T(8,128)S(1)} %get-tuple-element.121) | copy-start | bytes 165892
  126.6 46.3 %all-to-all-start.1 = ((bf16[3,12,96,384]{3,1,0,2:T(8,128)(2,1)}), bf16[3,12,96,384]{3,1,0,2:T(8,128)(2,1)}, u32[]{:S(2)}, u32[]{:S(2)}) async-start(bf16[3,12,96,384]{3,1,0,2:T(8,128)(2,1)} %copy.334), calls=%async_computation.1 | async-start | bytes 7077888 | tf_op jit(solution)/shard_map/all_to_all | solution.py:110
  133.4 343.9 %copy-start.50 = (f32[3,48,384]{2,1,0:T(8,128)}, f32[3,48,384]{2,1,0:T(8,128)S(1)}, u32[]{:S(2)}) copy-start(f32[3,48,384]{2,1,0:T(8,128)S(1)} %get-tuple-element.114) | copy-start | bytes 663556
  144.9 95.3 %copy-start.138 = (f32[48,32]{1,0:T(8,128)}, f32[48,32]{1,0:T(8,128)S(1)}, u32[]{:S(2)}) copy-start(f32[48,32]{1,0:T(8,128)S(1)} %get-tuple-element.132) | copy-start | bytes 18436
  144.9 95.3 %copy-start.140 = (f32[48,32]{1,0:T(8,128)}, f32[48,32]{1,0:T(8,128)S(1)}, u32[]{:S(2)}) copy-start(f32[48,32]{1,0:T(8,128)S(1)} %get-tuple-element.133) | copy-start | bytes 18436
  146.2 188.2 %copy-start.47 = (bf16[3,120,2,6,64]{1,4,3,2,0:T(8,128)(2,1)}, bf16[3,120,2,6,64]{1,4,3,2,0:T(8,128)(2,1)S(1)}, u32[]{:S(2)}) copy-start(bf16[3,120,2,6,64]{1,4,3,2,0:T(8,128)(2,1)S(1)} %convolution_convert_fusion.16) | copy-start | bytes 1658884
  172.9 193.8 %all-to-all-start = ((bf16[3,12,96,384]{3,1,0,2:T(8,128)(2,1)}), bf16[3,12,96,384]{3,1,0,2:T(8,128)(2,1)}, u32[]{:S(2)}, u32[]{:S(2)}) async-start(bf16[3,12,96,384]{3,1,0,2:T(8,128)(2,1)} %copy.322), calls=%async_computation | async-start | bytes 7077888 | tf_op jit(solution)/shard_map/all_to_all | solution.py:112
  219.6 20.6 %copy-start.31 = (f32[3,48,24,6]{2,3,1,0:T(8,128)}, f32[3,48,24,6]{2,3,1,0:T(8,128)S(1)}, u32[]{:S(2)}) copy-start(f32[3,48,24,6]{2,3,1,0:T(8,128)S(1)} %fusion.382) | copy-start | bytes 248836
  219.7 20.5 %copy-start.33 = (f32[3,48,24,6]{2,3,1,0:T(8,128)}, f32[3,48,24,6]{2,3,1,0:T(8,128)S(1)}, u32[]{:S(2)}) copy-start(f32[3,48,24,6]{2,3,1,0:T(8,128)S(1)} %fusion.383) | copy-start | bytes 248836
  369.9 58.2 %copy-start.10 = (f32[3,12,4,24,384]{4,3,1,2,0:T(8,128)}, f32[3,12,4,24,384]{4,3,1,2,0:T(8,128)S(1)}, u32[]{:S(2)}) copy-start(f32[3,12,4,24,384]{4,3,1,2,0:T(8,128)S(1)} %get-tuple-element.86) | copy-start | bytes 15925252
  483.5 28.0 %slice-start.12 = ((s8[5308416]{0:T(1024)(128)(4,1)}), s8[1114112]{0:T(1024)(128)(4,1)S(1)}, s32[]{:S(2)}) async-start(s8[5308416]{0:T(1024)(128)(4,1)} %bitcast.792), calls=%async_computation.16 | async-start | bytes 2228224
  520.3 31.3 %slice-start.26 = ((s8[5308416]{0:T(1024)(128)(4,1)}), s8[1114112]{0:T(1024)(128)(4,1)S(1)}, s32[]{:S(2)}) async-start(s8[5308416]{0:T(1024)(128)(4,1)} %bitcast.825), calls=%async_computation.30 | async-start | bytes 2228224
  532.5 19.1 %slice-start.27 = ((s8[5308416]{0:T(1024)(128)(4,1)}), s8[4194304]{0:T(1024)(128)(4,1)S(1)}, s32[]{:S(2)}) async-start(s8[5308416]{0:T(1024)(128)(4,1)} %bitcast.825), calls=%async_computation.31 | async-start | bytes 8388608
  593.2 24.5 %copy-start.29 = (f32[3,48,24,6]{2,3,1,0:T(8,128)S(1)}, f32[3,48,24,6]{2,3,1,0:T(8,128)}, u32[]{:S(2)}) copy-start(f32[3,48,24,6]{2,3,1,0:T(8,128)} %copy-done.28) | copy-start | bytes 248836
  593.2 25.9 %copy-start.27 = (f32[3,48,24,6]{2,3,1,0:T(8,128)S(1)}, f32[3,48,24,6]{2,3,1,0:T(8,128)}, u32[]{:S(2)}) copy-start(f32[3,48,24,6]{2,3,1,0:T(8,128)} %copy-done.26) | copy-start | bytes 248836
  593.2 26.1 %copy-start.32 = (f32[3,48,24,6]{2,3,1,0:T(8,128)S(1)}, f32[3,48,24,6]{2,3,1,0:T(8,128)}, u32[]{:S(2)}) copy-start(f32[3,48,24,6]{2,3,1,0:T(8,128)} %copy-done.31) | copy-start | bytes 248836
  593.2 26.1 %copy-start.34 = (f32[3,48,24,6]{2,3,1,0:T(8,128)S(1)}, f32[3,48,24,6]{2,3,1,0:T(8,128)}, u32[]{:S(2)}) copy-start(f32[3,48,24,6]{2,3,1,0:T(8,128)} %copy-done.33) | copy-start | bytes 248836
  617.7 29.9 %slice-start.20 = ((s8[5308416]{0:T(1024)(128)(4,1)}), s8[4194304]{0:T(1024)(128)(4,1)S(1)}, s32[]{:S(2)}) async-start(s8[5308416]{0:T(1024)(128)(4,1)} %bitcast.815), calls=%async_computation.24 | async-start | bytes 8388608
  619.4 28.3 %slice-start.21 = ((s8[5308416]{0:T(1024)(128)(4,1)}), s8[1114112]{0:T(1024)(128)(4,1)S(1)}, s32[]{:S(2)}) async-start(s8[5308416]{0:T(1024)(128)(4,1)} %bitcast.815), calls=%async_computation.25 | async-start | bytes 2228224
  619.4 40.5 %slice-start = ((s8[5308416]{0:T(1024)(128)(4,1)}), s8[4194304]{0:T(1024)(128)(4,1)S(1)}, s32[]{:S(2)}) async-start(s8[5308416]{0:T(1024)(128)(4,1)} %bitcast.775), calls=%async_computation.4 | async-start | bytes 8388608
  675.3 35.1 %all-to-all-start.2 = ((bf16[3,48,24,384]{3,2,0,1:T(8,128)(2,1)}), bf16[3,48,24,384]{3,2,0,1:T(8,128)(2,1)S(1)}, u32[]{:S(2)}, u32[]{:S(2)}) async-start(bf16[3,48,24,384]{3,2,0,1:T(8,128)(2,1)} %copy.363), calls=%async_computation.2 | async-start | bytes 5308416 | tf_op jit(solution)/shard_map/all_to_all | solution.py:114
  679.0 531.7 %all-reduce.29.cloned.1.call-start = ((), (), s32[]{:S(2)}) async-start(), calls=%async_computation.3 | async-start | bytes 37748736 | tf_op jit(solution)/shard_map/psum | solution.py:117
  685.8 24.6 %copy-start.133 = (f32[3,12,384]{2,0,1:T(4,128)S(1)}, f32[3,12,384]{2,0,1:T(4,128)}, u32[]{:S(2)}) copy-start(f32[3,12,384]{2,0,1:T(4,128)} %copy.365) | copy-start | bytes 165892
  712.0 18.3 %copy-start.89 = (f32[3,12,384]{2,1,0:T(8,128)S(1)}, f32[3,12,384]{2,1,0:T(8,128)}, u32[]{:S(2)}) copy-start(f32[3,12,384]{2,1,0:T(8,128)} %get-tuple-element.118) | copy-start | bytes 165892
  712.0 18.3 %copy-start.117 = (f32[3,12,96]{2,1,0:T(8,128)S(1)}, f32[3,12,96]{2,1,0:T(8,128)}, u32[]{:S(2)}) copy-start(f32[3,12,96]{2,1,0:T(8,128)} %copy-done.116) | copy-start | bytes 41476
  712.0 18.3 %copy-start.149 = (f32[3,12,96]{2,1,0:T(8,128)S(1)}, f32[3,12,96]{2,1,0:T(8,128)}, u32[]{:S(2)}) copy-start(f32[3,12,96]{2,1,0:T(8,128)} %copy-done.148) | copy-start | bytes 41476
  712.1 18.3 %copy-start.160 = (f32[3,12,384]{2,1,0:T(8,128)S(1)}, f32[3,12,384]{2,1,0:T(8,128)}, u32[]{:S(2)}) copy-start(f32[3,12,384]{2,1,0:T(8,128)} %get-tuple-element.117) | copy-start | bytes 165892
  848.1 18.3 %copy-start.54 = (f32[3,12,96,6]{2,3,1,0:T(8,128)S(1)}, f32[3,12,96,6]{2,3,1,0:T(8,128)}, u32[]{:S(2)}) copy-start(f32[3,12,96,6]{2,3,1,0:T(8,128)} %copy-done.53) | copy-start | bytes 248836
  848.1 18.3 %copy-start.65 = (bf16[1,384,1536]{2,1,0:T(8,128)(2,1)S(1)}, bf16[1,384,1536]{2,1,0:T(8,128)(2,1)}, u32[]{:S(2)}) copy-start(bf16[1,384,1536]{2,1,0:T(8,128)(2,1)} %fusion.231) | copy-start | bytes 3538948
  848.1 18.4 %copy-start.67 = (bf16[1,384,1536]{2,1,0:T(8,128)(2,1)S(1)}, bf16[1,384,1536]{2,1,0:T(8,128)(2,1)}, u32[]{:S(2)}) copy-start(bf16[1,384,1536]{2,1,0:T(8,128)(2,1)} %fusion.233) | copy-start | bytes 3538948
  (177 other events, 1244.8 us)
Sparse Core Ops, SparseCore 0:
  903.5 307.1 all-reduce.28
where the time goes:
time: 1240 us; the launch traced here: 1230 us
  matrix products  490 us (40%)
  other arithmetic  289 us (23%)
  waiting for transfers between devices  265 us (21%)
  local copies, waits for them, and re-layouts  117 us (9%)
  blocking collectives  41.4 us (3%)
  between operations  16.9 us (1%)
  starting transfers between devices  13.6 us (1%)
    psum x1, waiting for transfers between devices, local_step(): grads = lax.psum(grads, ('dp', 'sp'))  228 us
    dot_general x6, matrix products, block_rest(): mlp_out = jnp.dot(hidden, w_mlp_out, preferred_element_type=jnp.float32)  90.9 us
    dot_general x6, matrix products, attn_inputs(): jnp.einsum('btsd,dkhe->btskhe', normed, w_qkv, preferred_element_type=jnp...  66.7 us
    dot_general x6, matrix products, block_rest(): jnp.dot(normed, w_mlp_in, preferred_element_type=jnp.float32)  54.2 us
    psum x1, blocking collectives, local_step(): grads = lax.psum(grads, ('dp', 'sp'))  41.4 us
    broadcast_in_dim x2, other arithmetic, attn_inputs(): keys = rms_heads(qkv_all[:, :, :, 1])  38.9 us
    dot_general x3, matrix products, attn_core(): jnp.einsum('bshqk,bkshe->bqshe', attn_prob, values, preferred_element_typ...  38.3 us
    unnamed x421, local copies, waits for them, and re-layouts  37.9 us
  transfers between devices with their start and end apart: 4, of which 3 were waited for; matrix products, arithmetic and copies ran while one was open for 21% of the time, Pallas kernels for 0%

commit v1 on v0

v1 whole, which is shorter than its diff:
```python
import functools

import jax
import jax.numpy as jnp
from jax import lax
from jax.experimental import pallas as pl
from jax.experimental.pallas import tpu as pltpu
from jax.sharding import PartitionSpec as P

BF = jnp.bfloat16
F32 = jnp.float32
D = 384
HID = 1536
TILE = 384
GRP = 96
NG = TILE // GRP
TILES = 3
ROWS = TILE * TILES
CAP = 128
CH = 256
K0 = 0.7978845608028654
K1 = 0.044715
R_QKV, R_OUT, R_CQ, R_CKV, R_CO, R_MO, R_MOD, R_END = 0, 1152, 1536, 1920, 2688, 3072, 4608, 4656
VMEM_LIMIT = 66 * 1000 * 1000


def dnn(a, b):
    return lax.dot_general(a, b, (((1,), (0,)), ((), ())), preferred_element_type=F32)


def dnt(a, b):
    return lax.dot_general(a, b, (((1,), (1,)), ((), ())), preferred_element_type=F32)


def dtn(a, b):
    return lax.dot_general(a, b, (((0,), (0,)), ((), ())), preferred_element_type=F32)


def layer_norm(x):
    centered = x - jnp.mean(x, axis=-1, keepdims=True)
    rstd = lax.rsqrt(jnp.mean(centered * centered, axis=-1, keepdims=True) + 1e-6)
    return centered * rstd, rstd


def layer_norm_bwd(grad, normed, rstd):
    mean_g = jnp.mean(grad, axis=-1, keepdims=True)
    mean_gn = jnp.mean(grad * normed, axis=-1, keepdims=True)
    return rstd * (grad - mean_g - normed * mean_gn)


def rows8(x):
    return jnp.sum(x.reshape(x.shape[0] // 8, 8, x.shape[1]), axis=0)


def lane_low(rows):
    return lax.broadcasted_iota(jnp.int32, (rows, 128), 1) < 64


def head_sum_matrix():
    row = lax.broadcasted_iota(jnp.int32, (256, 128), 0)
    col = lax.broadcasted_iota(jnp.int32, (256, 128), 1)
    return jnp.where((row % 128) // 64 == col // 64, 1.0, 0.0).astype(BF)


def head_sum(x, ones):
    hi = x.astype(BF)
    lo = (x - hi.astype(F32)).astype(BF)
    return dnn(jnp.concatenate([hi, lo], axis=1), ones)


def swap_halves(x):
    lane = lax.broadcasted_iota(jnp.int32, x.shape, 1)
    return jnp.where(lane % 64 < 32, pltpu.roll(x, 96, 1), pltpu.roll(x, 32, 1))


def stack_heads(x, low, high):
    return jnp.concatenate([x * low, x * high], axis=0)


def pick_heads(x2, rows):
    return jnp.where(lane_low(rows), x2[:rows], x2[rows:])


def block_kernel(temporal, backward, len_ref, *refs):
    refs = list(refs)
    take = refs.pop
    x_ref = take(0)
    g_ref = take(0) if backward else None
    mods_ref, msk_ref, cap_ref = take(0), take(0), take(0)
    wqkv, wout, wcq, wckv, wco, win, wmo = [take(0) for _ in range(7)]
    if temporal:
        cos_ref, sin_ref, perm_ref = take(0), take(0), take(0)
    out_ref = take(0)
    if backward:
        acc_ref, accw_ref = take(0), take(0)
    qb_ref, vb_ref, kv_ref, m_ref = take(0), take(0), take(0), take(0)
    h_s, o_s, x1_s, oc_s, n_s = [take(0) for _ in range(5)]
    if backward:
        hid_s, dm_s, du_s, dx2_s, dqc_s, da_s, dqkv_s = [take(0) for _ in range(7)]
        qn_ref, rq_ref, ps_ref, pc_ref, a_ref, dn_ref, dkv_ref, do_ref, dqk_ref = [take(0) for _ in range(9)]

    s = pl.program_id(0)
    t = pl.program_id(1)
    r0 = pl.multiple_of(t * TILE, TILE) if backward else 0
    here = pl.ds(r0, TILE)
    lane_row = lax.broadcasted_iota(jnp.int32, (1, 128), 1)
    low = jnp.where(lane_row < 64, 1.0, 0.0).astype(BF)
    high = jnp.where(lane_row < 64, 0.0, 1.0).astype(BF)
    ones = head_sum_matrix()
    cond = msk_ref[0, 0] > 0.5

    def mod(index):
        return jnp.where(cond, mods_ref[0, index:index + 1, :], mods_ref[0, 8 + index:9 + index, :])

    if backward:
        @pl.when((s == 0) & (t == 0))
        def _():
            acc_ref[...] = jnp.zeros_like(acc_ref)
            accw_ref[...] = jnp.zeros_like(accw_ref)

    @pl.when(t == 0)
    def _():
        kv_ref[...] = dnt(cap_ref[0], wckv[0]).astype(BF)
        if backward:
            dkv_ref[...] = jnp.zeros_like(dkv_ref)

    def load_x():
        if temporal:
            return dnn(perm_ref[...], x_ref[...].reshape(TILE, D))
        return x_ref[...].reshape(TILE, D).astype(F32)

    normed, _ = layer_norm(load_x())
    h = (normed * (1.0 + mod(1)) + mod(0)).astype(BF)
    h_s[here, :] = h
    qkv = dnt(h, wqkv[0])
    for j in range(6):
        cols = slice(j * 128, (j + 1) * 128)
        raw = qkv[:, cols]
        inv = lax.rsqrt(head_sum(raw * raw, ones) * (1.0 / 64) + 1e-6)
        unit = raw * inv
        if backward:
            qn_ref[:, cols] = unit
            rq_ref[:, cols] = inv
        if temporal:
            unit = unit * cos_ref[...] + swap_halves(unit) * sin_ref[...]
        qb_ref[:, cols] = unit.astype(BF)
    vb_ref[...] = qkv[:, 2 * D:].astype(BF)

    if temporal:
        same = (lax.broadcasted_iota(jnp.int32, (2 * GRP, GRP), 0) // 48) % 2 == lax.broadcasted_iota(jnp.int32, (2 * GRP, GRP), 1) // 48

    def self_fwd(grp, carry):
        rows = pl.ds(pl.multiple_of(grp * GRP, GRP), GRP)
        for p in range(3):
            cols = slice(p * 128, (p + 1) * 128)
            kcols = slice(D + p * 128, D + (p + 1) * 128)
            q2 = stack_heads(qb_ref[rows, cols], low, high)
            e = jnp.exp(dnt(q2, qb_ref[rows, kcols]) * 0.125)
            if temporal:
                e = jnp.where(same, e, 0.0)
            prob = e * (1.0 / jnp.sum(e, axis=-1, keepdims=True))
            if backward:
                ps_ref[grp * 3 + p] = prob
            o2 = dnn(prob.astype(BF), vb_ref[rows, cols])
            o_s[pl.ds(pl.multiple_of(r0 + grp * GRP, GRP), GRP), cols] = pick_heads(o2, GRP).astype(BF)
        return carry

    lax.fori_loop(0, NG, self_fwd, 0)

    attn = dnn(o_s[here, :], wout[0])
    if backward:
        a_ref[...] = attn
    x1 = (load_x() + mod(2) * attn).astype(BF)
    x1_s[here, :] = x1

    qc = dnt(x1, wcq[0]).astype(BF)
    valid = lax.broadcasted_iota(jnp.int32, (2 * TILE, CAP), 1) < len_ref[s]
    for p in range(3):
        cols = slice(p * 128, (p + 1) * 128)
        q2 = stack_heads(qc[:, cols], low, high)
        sc = jnp.where(valid, dnt(q2, kv_ref[:, cols]) * 0.125, -1e30)
        e = jnp.exp(sc - jnp.max(sc, axis=-1, keepdims=True))
        prob = e * (1.0 / jnp.sum(e, axis=-1, keepdims=True))
        if backward:
            pc_ref[p] = prob
            dqc_s[here, cols] = qc[:, cols]
        o2 = dnn(prob.astype(BF), kv_ref[:, D + p * 128:D + (p + 1) * 128])
        oc_s[here, cols] = pick_heads(o2, TILE).astype(BF)
    x2 = (x1.astype(F32) + dnn(oc_s[here, :], wco[0])).astype(BF).astype(F32)

    normed2, rstd2 = layer_norm(x2)
    n_s[here, :] = (normed2 * (1.0 + mod(4)) + mod(3)).astype(BF)
    m_ref[...] = jnp.zeros_like(m_ref)

    if not backward:
        def mlp_fwd(c, carry):
            cols = pl.ds(pl.multiple_of(c * CH, CH), CH)
            u = dnn(n_s[here, :], win[0, :, cols])
            hid = (0.5 * u * (1.0 + jnp.tanh(K0 * (u + K1 * u * u * u)))).astype(BF)
            m_ref[...] += dnn(hid, wmo[0, cols, :])
            return carry

        lax.fori_loop(0, HID // CH, mlp_fwd, 0)
        x3 = x2 + mod(5) * m_ref[...]
        for f in range(4):
            for j in range(4):
                lo = f * 96 + j * 24
                out_ref[j, 0, f] = x3[lo:lo + 24].astype(BF)
        return

    def load_g():
        if temporal:
            return dnn(perm_ref[...], g_ref[...].reshape(TILE, D))
        return jnp.concatenate([g_ref[j, 0, f].astype(F32) for f in range(4) for j in range(4)], axis=0)

    g = load_g()
    dm_s[here, :] = (mod(5) * g).astype(BF)
    dn_ref[...] = jnp.zeros_like(dn_ref)

    def mlp_both(c, carry):
        cols = pl.ds(pl.multiple_of(c * CH, CH), CH)
        u = dnn(n_s[here, :], win[0, :, cols])
        u2 = u * u
        th = jnp.tanh(K0 * (u + K1 * u * u2))
        half = 0.5 * (1.0 + th)
        hid = (u * half).astype(BF)
        hid_s[here, cols] = hid
        slope = half + 0.5 * K0 * u * (1.0 - th * th) * (1.0 + 3.0 * K1 * u2)
        m_ref[...] += dnn(hid, wmo[0, cols, :])
        du = (dnt(dm_s[here, :], wmo[0, cols, :]) * slope).astype(BF)
        du_s[here, cols] = du
        dn_ref[...] += dnt(du, win[0, :, cols])
        return carry

    lax.fori_loop(0, HID // CH, mlp_both, 0)

    def add_mod(index, value):
        acc_ref[R_MOD + 8 * index:R_MOD + 8 * index + 8, :] += rows8(value)

    add_mod(5, g * m_ref[...])
    dn = dn_ref[...]
    add_mod(3, dn)
    add_mod(4, dn * normed2)
    dx2 = (g + layer_norm_bwd(dn * (1.0 + mod(4)), normed2, rstd2)).astype(BF)
    dx2_s[here, :] = dx2

    do_ref[...] = dnt(dx2, wco[0]).astype(BF)
    for p in range(3):
        cols = slice(p * 128, (p + 1) * 128)
        vcols = slice(D + p * 128, D + (p + 1) * 128)
        q2 = stack_heads(dqc_s[here, cols], low, high)
        do2 = stack_heads(do_ref[:, cols], low, high)
        prob = pc_ref[p]
        dp = dnt(do2, kv_ref[:, vcols])
        ds = (prob * (dp - jnp.sum(prob * dp, axis=-1, keepdims=True)) * 0.125).astype(BF)
        dqc_s[here, cols] = pick_heads(dnn(ds, kv_ref[:, cols]), TILE).astype(BF)
        dkv_ref[:, cols] += dtn(ds, q2)
        dkv_ref[:, vcols] += dtn(prob.astype(BF), do2)
    dx1 = (dx2.astype(F32) + dnn(dqc_s[here, :], wcq[0])).astype(BF)
    dx1f = dx1.astype(F32)

    add_mod(2, dx1f * a_ref[...])
    da = (mod(2) * dx1f).astype(BF)
    da_s[here, :] = da
    do_ref[...] = dnt(da, wout[0]).astype(BF)

    def self_bwd(grp, carry):
        rows = pl.ds(pl.multiple_of(grp * GRP, GRP), GRP)
        for p in range(3):
            cols = slice(p * 128, (p + 1) * 128)
            kcols = slice(D + p * 128, D + (p + 1) * 128)
            q2 = stack_heads(qb_ref[rows, cols], low, high)
            do2 = stack_heads(do_ref[rows, cols], low, high)
            prob = ps_ref[grp * 3 + p]
            dp = dnt(do2, vb_ref[rows, cols])
            ds = (prob * (dp - jnp.sum(prob * dp, axis=-1, keepdims=True)) * 0.125).astype(BF)
            dqk_ref[rows, cols] = pick_heads(dnn(ds, qb_ref[rows, kcols]), GRP)
            dqk_ref[rows, kcols] = dtn(ds, q2)
            dqkv_s[pl.ds(pl.multiple_of(r0 + grp * GRP, GRP), GRP), 2 * D + p * 128:2 * D + (p + 1) * 128] = dtn(prob.astype(BF), do2).astype(BF)
        return carry

    lax.fori_loop(0, NG, self_bwd, 0)
    for j in range(6):
        cols = slice(j * 128, (j + 1) * 128)
        grad = dqk_ref[:, cols]
        if temporal:
            grad = grad * cos_ref[...] - swap_halves(grad) * sin_ref[...]
        unit = qn_ref[:, cols]
        mean = head_sum(grad * unit, ones) * (1.0 / 64)
        dqkv_s[here, cols] = (rq_ref[:, cols] * (grad - unit * mean)).astype(BF)
    dh = dnn(dqkv_s[here, :], wqkv[0])
    normed, rstd = layer_norm(load_x())
    add_mod(0, dh)
    add_mod(1, dh * normed)
    dx = dx1f + layer_norm_bwd(dh * (1.0 + mod(1)), normed, rstd)
    if temporal:
        back = dtn(perm_ref[...], dx.astype(BF))
        out_ref[...] = back.astype(BF).reshape(4, 1, 12, 8, D)
    else:
        out_ref[...] = dx.astype(BF).reshape(1, 4, 96, D)

    @pl.when(t == TILES - 1)
    def _():
        acc_ref[R_OUT:R_CQ, :] += dtn(o_s[...], da_s[...])
        acc_ref[R_CQ:R_CKV, :] += dtn(dqc_s[...], x1_s[...])
        acc_ref[R_CKV:R_CO, :] += dtn(dkv_ref[...].astype(BF), cap_ref[0])
        acc_ref[R_CO:R_MO, :] += dtn(oc_s[...], dx2_s[...])

        def qkv_rows(c, carry):
            rows = pl.ds(pl.multiple_of(R_QKV + c * D, 128), D)
            acc_ref[rows, :] += dtn(dqkv_s[:, pl.ds(pl.multiple_of(c * D, 128), D)], h_s[...])
            return carry

        lax.fori_loop(0, 3, qkv_rows, 0)

        def mlp_rows(c, carry):
            cols = pl.ds(pl.multiple_of(c * 512, 512), 512)
            acc_ref[pl.ds(pl.multiple_of(R_MO + c * 512, 512), 512), :] += dtn(hid_s[:, cols], dm_s[...])
            accw_ref[:, cols] += dtn(n_s[...], du_s[:, cols])
            return carry

        lax.fori_loop(0, 3, mlp_rows, 0)


def run_block(index, temporal, backward, x, g, shared):
    mods, msk, cap, lens, weights, tables = shared
    samples = cap.shape[0]
    spatial_block = pl.BlockSpec((1, 4, 96, D), lambda s, t: (s, t, 0, 0))
    split_block = pl.BlockSpec((4, 1, 4, 24, D), lambda s, t: (0, s, t, 0, 0))
    cols_block = pl.BlockSpec((4, 1, 12, 8, D), lambda s, t: (0, s, 0, t, 0))

    def const(shape, first=0):
        return pl.BlockSpec(shape, lambda s, t: (first,) + (0,) * (len(shape) - 1), pipeline_mode=pl.Buffered(1))

    in_specs = [pl.BlockSpec(memory_space=pltpu.SMEM), cols_block if temporal else spatial_block]
    operands = [lens, x]
    if backward:
        in_specs.append(cols_block if temporal else split_block)
        operands.append(g)
    in_specs += [
        pl.BlockSpec((1, 16, D), lambda s, t: (s, 0, 0)),
        pl.BlockSpec((1, 1, TILE, 1), lambda s, t: (s, t, 0, 0)),
        pl.BlockSpec((1, CAP, D), lambda s, t: (s, 0, 0)),
    ]
    operands += [mods, msk, cap]
    for weight in weights:
        in_specs.append(const((1,) + weight.shape[1:], index))
        operands.append(weight)
    if temporal:
        for table in tables:
            in_specs.append(const(table.shape))
            operands.append(table)

    def vm(rows, cols, dtype=BF):
        return pltpu.VMEM((rows, cols), dtype)

    keep = ROWS if backward else TILE
    scratch = [vm(TILE, 2 * D), vm(TILE, D), vm(CAP, 2 * D), vm(TILE, D, F32)] + [vm(keep, D)] * 5
    split_shape = jax.ShapeDtypeStruct((4, samples, 12, 24, D), BF)
    if backward:
        out_shape = [
            split_shape if temporal else jax.ShapeDtypeStruct((samples, 12, 96, D), BF),
            jax.ShapeDtypeStruct((R_END, D), F32),
            jax.ShapeDtypeStruct((D, HID), F32),
        ]
        out_specs = [
            cols_block if temporal else spatial_block,
            pl.BlockSpec((R_END, D), lambda s, t: (0, 0), pipeline_mode=pl.Buffered(1)),
            pl.BlockSpec((D, HID), lambda s, t: (0, 0), pipeline_mode=pl.Buffered(1)),
        ]
        scratch += [vm(ROWS, HID), vm(ROWS, D), vm(ROWS, HID), vm(ROWS, D), vm(ROWS, D), vm(ROWS, D), vm(ROWS, 3 * D)]
        scratch += [
            vm(TILE, 2 * D, F32), vm(TILE, 2 * D, F32),
            pltpu.VMEM((3 * NG, 2 * GRP, GRP), F32), pltpu.VMEM((3, 2 * TILE, CAP), F32),
            vm(TILE, D, F32), vm(TILE, D, F32), vm(CAP, 2 * D, F32), vm(TILE, D), vm(TILE, 2 * D, F32),
        ]
    else:
        out_shape = split_shape
        out_specs = split_block
    flops = samples * ROWS * (13 if backward else 4.6) * 1e6
    return pl.pallas_call(
        functools.partial(block_kernel, temporal, backward),
        grid=(samples, TILES),
        in_specs=in_specs,
        out_specs=out_specs,
        out_shape=out_shape,
        scratch_shapes=scratch,
        compiler_params=pltpu.CompilerParams(
            dimension_semantics=("arbitrary", "arbitrary"), vmem_limit_bytes=VMEM_LIMIT),
        cost_estimate=pl.CostEstimate(flops=int(flops), bytes_accessed=20_000_000, transcendentals=0),
        name=("temporal" if temporal else "spatial") + ("_bwd" if backward else "_fwd"),
    )(*operands)


def rotary_tables():
    row_frame = jnp.arange(TILE) % 48
    inv_freq = 10000.0 ** (-jnp.arange(32, dtype=F32) / 32)
    angle = row_frame.astype(F32)[:, None] * inv_freq[None, :]
    cosine = jnp.tile(jnp.cos(angle), (1, 4))
    sine = jnp.sin(angle)
    signed = jnp.tile(jnp.concatenate([-sine, sine], axis=1), (1, 2))
    source = (jnp.arange(TILE) % 48) * 8 + jnp.arange(TILE) // 48
    perm = (source[:, None] == jnp.arange(TILE)[None, :]).astype(BF)
    return cosine, signed, perm


def solution(mesh):
    tok_spec = P('dp', 'sp')
    row_spec = P('dp')
    in_specs = (tok_spec, row_spec, row_spec, row_spec, row_spec, row_spec, P(), P(), P(), P(), P(), P(), P(), P(), tok_spec)
    out_specs = (tok_spec, P(), P(), P(), P(), P(), P(), P(), P())

    def local_step(latents, t_mod, t_mod_zero, frame_mask, captions, caption_len, w_qkv, w_out, w_cross_q, w_cross_kv, w_cross_out, w_mlp_in, w_mlp_out, mod_table, grad_out):
        samples = latents.shape[0]
        exchange = functools.partial(lax.all_to_all, axis_name='sp', split_axis=0, concat_axis=0, tiled=True)
        grad_split = jnp.moveaxis(grad_out.reshape(samples, 12, 4, 24, D), 2, 0)
        grad_cols = exchange(grad_split)
        weights = (
            jnp.transpose(w_qkv, (0, 2, 3, 4, 1)).reshape(2, 3 * D, D),
            w_out.reshape(2, D, D),
            jnp.transpose(w_cross_q, (0, 2, 3, 1)).reshape(2, D, D),
            jnp.transpose(w_cross_kv, (0, 2, 3, 4, 1)).reshape(2, 2 * D, D),
            w_cross_out.reshape(2, D, D),
            w_mlp_in,
            w_mlp_out,
        )
        cap = jnp.pad(captions, ((0, 0), (0, CAP - captions.shape[1]), (0, 0)))
        pad2 = ((0, 0), (0, 2), (0, 0))

        def mods_of(index):
            return jnp.concatenate([jnp.pad(mod_table[index] + t_mod, pad2), jnp.pad(mod_table[index] + t_mod_zero, pad2)], axis=1)

        mask = frame_mask.astype(F32)
        local_mask = lax.dynamic_slice_in_dim(mask, lax.axis_index('sp') * 12, 12, axis=1)
        msk_rows = jnp.repeat(local_mask, 96, axis=1).reshape(samples, TILES, TILE, 1)
        msk_cols = jnp.tile(mask, (1, 24)).reshape(samples, TILES, TILE, 1)
        tables = rotary_tables()
        shared0 = (mods_of(0), msk_rows, cap, caption_len, weights, tables)
        shared1 = (mods_of(1), msk_cols, cap, caption_len, weights, tables)

        middle = run_block(0, False, False, latents, None, shared0)
        dmid, acc1, accw1 = run_block(1, True, True, exchange(middle), grad_cols, shared1)
        sum1 = lax.psum((acc1, accw1), ('dp', 'sp'))
        grad_latents, acc0, accw0 = run_block(0, False, True, latents, exchange(dmid), shared0)
        acc0, accw0, sum1 = lax.optimization_barrier((acc0, accw0, sum1))
        sum0 = lax.psum((acc0, accw0), ('dp', 'sp'))

        def rows(first, last):
            return jnp.stack([sum0[0][first:last], sum1[0][first:last]])

        g_qkv = jnp.transpose(rows(R_QKV, R_OUT).reshape(2, 3, 6, 64, D), (0, 4, 1, 2, 3))
        g_out = rows(R_OUT, R_CQ).reshape(2, 6, 64, D)
        g_cq = jnp.transpose(rows(R_CQ, R_CKV).reshape(2, 6, 64, D), (0, 3, 1, 2))
        g_ckv = jnp.transpose(rows(R_CKV, R_CO).reshape(2, 2, 6, 64, D), (0, 4, 1, 2, 3))
        g_co = rows(R_CO, R_MO).reshape(2, 6, 64, D)
        g_mo = rows(R_MO, R_MOD)
        g_mi = jnp.stack([sum0[1], sum1[1]])
        g_mod = jnp.sum(rows(R_MOD, R_END).reshape(2, 6, 8, D), axis=2)
        return grad_latents, g_qkv, g_out, g_cq, g_ckv, g_co, g_mi, g_mo, g_mod

    return jax.shard_map(local_step, mesh=mesh, in_specs=in_specs, out_specs=out_specs, check_vma=False)
```

time: 1240 us -> 879 us (0.71)
  Pallas kernels: 0 us -> 518 us
  matrix products: 490 us -> 0 us
  other arithmetic: 289 us -> 16 us
  local copies, waits for them, and re-layouts: 117 us -> 29.6 us
  blocking collectives: 41.4 us -> 0 us
  waiting for transfers between devices: 265 us -> 286 us
    pallas_call x0 -> x3, Pallas kernels: none -> 518 us  [run_block(): pl.pallas_call(functools.partial(block_kernel, temporal, backward), grid=...]
    dot_general x61 -> x0, matrix products: 463 us -> none  [the longest x6 90.9 us: block_rest(): mlp_out = jnp.dot(hidden, w_mlp_out, preferred_element_type=jnp.float32)]
    reduce_sum x18 -> x1, other arithmetic: 75 us -> 0.04 us  [local_step(): g_mod = jnp.sum(rows(R_MOD, R_END).reshape(2, 6, 8, D), axis=2)]
    all_to_all x3, waiting for transfers between devices: 36.5 us -> 101 us  [the longest x1 45 us: local_step(): exchange(dmid)]
    psum x1 -> x2, waiting for transfers between devices: 228 us -> 185 us  [the longest x1 185 us: local_step(): sum0 = lax.psum((acc0, accw0), ('dp', 'sp'))]
    psum x1 -> x0, blocking collectives: 41.4 us -> none  [local_step(): grads = lax.psum(grads, ('dp', 'sp'))]
    broadcast_in_dim x3 -> x0, other arithmetic: 39 us -> none  [the longest x2 38.9 us: attn_inputs(): keys = rms_heads(qkv_all[:, :, :, 1])]
    unnamed x421 -> x19, local copies, waits for them, and re-layouts: 37.9 us -> 1.88 us
  transfers between devices with their start and end apart: 4 -> 5, of which waited for: 3 -> 4; matrix products, arithmetic and copies ran while one was open for 21% -> 2% of each run, Pallas kernels for 0% -> 23%
where the time goes in v1:
time: 879 us; the launch traced here: 878 us
  Pallas kernels  518 us (59%)
  waiting for transfers between devices  286 us (33%)
  local copies, waits for them, and re-layouts  29.6 us (3%)
  other arithmetic  16 us (2%)
  between operations  14.2 us (2%)
  starting transfers between devices  14.1 us (2%)
    pallas_call x3, Pallas kernels, run_block(): pl.pallas_call(functools.partial(block_kernel, temporal, backward), grid=...  518 us
    psum x1, waiting for transfers between devices, local_step(): sum0 = lax.psum((acc0, accw0), ('dp', 'sp'))  185 us
    all_to_all x1, waiting for transfers between devices, local_step(): exchange(dmid)  45 us
    all_to_all x1, waiting for transfers between devices, local_step(): exchange(middle)  30.3 us
    all_to_all x1, waiting for transfers between devices, local_step(): grad_cols = exchange(grad_split)  25.8 us
  transfers between devices with their start and end apart: 5, of which 4 were waited for; matrix products, arithmetic and copies ran while one was open for 2% of the time, Pallas kernels for 23%

profile of v1, /device:TPU:0, one launch (start us, length us, event | category | flops | bytes accessed | tf_op | source)
XLA Modules:
  0.0 878.0 jit_solution(14076579896913395044)
XLA Ops:
  8.9 2.9 reshape_reshape.4.refs_2_.refs_3_
  14.0 91.4 %spatial_fwd.1 = bf16[4,3,12,24,384]{4,3,2,1,0:T(8,128)(2,1)} custom-call(s32[3]{0:T(128)} %len_ref.5, bf16[3,12,96,384]{3,2,1,0:T(8,128)(2,1)} %refs_0_.3, f32[3,16,384]{2,1,0:T(8,128)} %select_maximum_fusion.1.refs_1_.refs_2_, f32[3,3,384,1]{3,2,1,0:T(8,128)} %reshape_reshape.4.refs_2_.refs_3_, bf16[3,128,384]{2,1,0:T(8,128)(2,1)} %pad.19.refs_3_.refs_4_, ...), custom_call_target="tpu_custom_call" | custom-call | flops 15897600000 | bytes 20000000 | tf_op jit(solution)/shard_map/spatial_fwd/pallas_call | solution.py:381
  105.4 4.8 all-to-all-start
  110.2 1.8 copy.46
  112.0 30.3 %all-to-all-done.refs_0_ = bf16[4,3,12,24,384]{4,3,2,1,0:T(8,128)(2,1)} async-done(((bf16[4,3,12,24,384]{4,3,2,1,0:T(8,128)(2,1)}), bf16[4,3,12,24,384]{4,3,2,1,0:T(8,128)(2,1)}, u32[]{:S(2)}, u32[]{:S(2)}) %all-to-all-start) | async-done | bytes 2654240 | tf_op jit(solution)/shard_map/all_to_all | solution.py:442
  142.3 4.6 all-to-all-start.1
  147.2 0.8 copy.38.refs_13_
  148.9 2.1 tile.32.refs_3_
  151.6 0.8 fusion.refs_14_
  152.5 25.8 %all-to-all-done.1.refs_1_ = bf16[4,3,12,24,384]{4,3,2,1,0:T(8,128)(2,1)} async-done(((bf16[4,3,12,24,384]{4,3,2,1,0:T(8,128)(2,1)}), bf16[4,3,12,24,384]{4,3,2,1,0:T(8,128)(2,1)}, u32[]{:S(2)}, u32[]{:S(2)}) %all-to-all-start.1) | async-done | bytes 2654240 | tf_op jit(solution)/shard_map/all_to_all | solution.py:417
  178.3 220.8 %temporal_bwd.1 = (bf16[4,3,12,24,384]{4,3,2,1,0:T(8,128)(2,1)}, f32[4656,384]{1,0:T(8,128)}, f32[384,1536]{1,0:T(8,128)}) custom-call(s32[3]{0:T(128)} %len_ref.5, bf16[4,3,12,24,384]{4,3,2,1,0:T(8,128)(2,1)} %all-to-all-done.refs_0_, bf16[4,3,12,24,384]{4,3,2,1,0:T(8,128)(2,1)} %all-to-all-done.1.refs_1_, f32[3,16,384]{2,1,0:T(8,128)} %select_maximum_fusion.refs_2_, ...), custom_call_target="tpu_custom_call" | custom-call | flops 44928000000 | bytes 20000000 | tf_op jit(solution)/shard_map/temporal_bwd/pallas_call | solution.py:381
  399.1 4.6 all-to-all-start.2
  404.4 45.0 %all-to-all-done.2.refs_1_ = bf16[4,3,12,24,384]{4,3,2,1,0:T(8,128)(2,1)} async-done(((bf16[4,3,12,24,384]{4,3,2,1,0:T(8,128)(2,1)}), bf16[4,3,12,24,384]{4,3,2,1,0:T(8,128)(2,1)}, u32[]{:S(2)}, u32[]{:S(2)}) %all-to-all-start.2) | async-done | bytes 2654240 | tf_op jit(solution)/shard_map/all_to_all | solution.py:444
  449.4 205.5 %spatial_bwd.1 = (bf16[3,12,96,384]{3,2,1,0:T(8,128)(2,1)}, f32[4656,384]{1,0:T(8,128)}, f32[384,1536]{1,0:T(8,128)}) custom-call(s32[3]{0:T(128)} %len_ref.5, bf16[3,12,96,384]{3,2,1,0:T(8,128)(2,1)} %refs_0_.3, bf16[4,3,12,24,384]{4,3,2,1,0:T(8,128)(2,1)} %all-to-all-done.2.refs_1_, f32[3,16,384]{2,1,0:T(8,128)} %select_maximum_fusion.1.refs_1_.refs_2_, ...), custom_call_target="tpu_custom_call" | custom-call | flops 44928000000 | bytes 20000000 | tf_op jit(solution)/shard_map/spatial_bwd/pallas_call | solution.py:381
  655.0 1.3 slice.59
  656.3 2.8 slice.53
  659.1 1.5 slice_bitcast_fusion.3
  660.6 2.7 fusion.10
  663.3 1.8 slice_bitcast_fusion.1
  665.1 184.6 %all-reduce.10.cloned.1.call-done = (f32[4656,384]{1,0:T(8,128)}, f32[1,384,1536]{2,1,0:T(8,128)}) async-done(((f32[4656,384]{1,0:T(8,128)}, f32[1,384,1536]{2,1,0:T(8,128)}), (f32[4656,384]{1,0:T(8,128)}, f32[1,384,1536]{2,1,0:T(8,128)})) %all-reduce.10.cloned.1.call-update) | async-done | bytes 9510928 | tf_op jit(solution)/shard_map/psum | solution.py:446
  849.8 0.9 slice_bitcast_fusion.2
  850.6 1.3 slice.69
  852.0 1.6 slice.66
  853.6 1.6 fusion.9
  855.2 2.0 slice_bitcast_fusion
  858.3 2.5 pad_maximum_fusion
  860.8 1.6 maximum_bitcast_fusion.1
  863.1 2.2 maximum_bitcast_fusion
  865.2 2.5 pad_maximum_fusion.1
  867.7 1.1 pad_maximum_fusion.3
  868.9 1.1 maximum_bitcast_fusion.2
  870.0 1.1 pad_maximum_fusion.2
  (43 shorter events, 8.4 us)
Async XLA Ops:
  7.2 6.1 copy-start.8
  105.4 4.9 copy-start.1
  105.4 36.9 %all-to-all-start = ((bf16[4,3,12,24,384]{4,3,2,1,0:T(8,128)(2,1)}), bf16[4,3,12,24,384]{4,3,2,1,0:T(8,128)(2,1)}, u32[]{:S(2)}, u32[]{:S(2)}) async-start(bf16[4,3,12,24,384]{4,3,2,1,0:T(8,128)(2,1)} %spatial_fwd.1), calls=%async_computation | async-start | bytes 5308416 | tf_op jit(solution)/shard_map/all_to_all | solution.py:442
  142.3 36.0 %all-to-all-start.1 = ((bf16[4,3,12,24,384]{4,3,2,1,0:T(8,128)(2,1)}), bf16[4,3,12,24,384]{4,3,2,1,0:T(8,128)(2,1)}, u32[]{:S(2)}, u32[]{:S(2)}) async-start(bf16[4,3,12,24,384]{4,3,2,1,0:T(8,128)(2,1)} %bitcast.46), calls=%async_computation.1 | async-start | bytes 5308416 | tf_op jit(solution)/shard_map/all_to_all | solution.py:417
  399.1 50.3 %all-to-all-start.2 = ((bf16[4,3,12,24,384]{4,3,2,1,0:T(8,128)(2,1)}), bf16[4,3,12,24,384]{4,3,2,1,0:T(8,128)(2,1)}, u32[]{:S(2)}, u32[]{:S(2)}) async-start(bf16[4,3,12,24,384]{4,3,2,1,0:T(8,128)(2,1)} %get-tuple-element.19), calls=%async_computation.2 | async-start | bytes 5308416 | tf_op jit(solution)/shard_map/all_to_all | solution.py:444
  403.6 251.3 %all-reduce.12.cloned.1.call-start = ((), (), s32[]{:S(2)}) async-start(), calls=%async_computation.4 | async-start | bytes 19021824 | tf_op jit(solution)/shard_map/psum | solution.py:443
  404.4 445.4 %all-reduce.10.cloned.1.call-start = ((), (), s32[]{:S(2)}) async-start(), calls=%async_computation.3 | async-start | bytes 19021824 | tf_op jit(solution)/shard_map/psum | solution.py:446
  853.6 3.6 copy-start.7
  855.2 2.7 copy-start.5
  855.2 3.1 copy-start.6
  860.8 2.3 copy-start
  865.2 2.5 copy-start.4
  867.7 1.2 copy-start.3
  867.7 2.3 copy-start.2
Sparse Core Ops, SparseCore 0:
  411.0 198.9 all-reduce.11
  655.1 194.6 all-reduce.9

commit v2 on v1

--- a/solution.py
+++ b/solution.py
@@ -17,7 +17,7 @@
 TILES = 3
 ROWS = TILE * TILES
 CAP = 128
-CH = 256
+CH = 512
 K0 = 0.7978845608028654
 K1 = 0.044715
 R_QKV, R_OUT, R_CQ, R_CKV, R_CO, R_MO, R_MOD, R_END = 0, 1152, 1536, 1920, 2688, 3072, 4608, 4656
@@ -81,7 +81,7 @@
     return jnp.where(lane_low(rows), x2[:rows], x2[rows:])
 
 
-def block_kernel(temporal, backward, len_ref, *refs):
+def block_kernel(temporal, backward, first, chained, len_ref, *refs):
     refs = list(refs)
     take = refs.pop
     x_ref = take(0)
@@ -90,6 +90,8 @@
     wqkv, wout, wcq, wckv, wco, win, wmo = [take(0) for _ in range(7)]
     if temporal:
         cos_ref, sin_ref, perm_ref = take(0), take(0), take(0)
+    if chained:
+        acc_in, accw_in = take(0), take(0)
     out_ref = take(0)
     if backward:
         acc_ref, accw_ref = take(0), take(0)
@@ -115,8 +117,12 @@
     if backward:
         @pl.when((s == 0) & (t == 0))
         def _():
-            acc_ref[...] = jnp.zeros_like(acc_ref)
-            accw_ref[...] = jnp.zeros_like(accw_ref)
+            if chained:
+                pltpu.sync_copy(acc_in, acc_ref)
+                pltpu.sync_copy(accw_in, accw_ref)
+            else:
+                acc_ref[...] = jnp.zeros_like(acc_ref)
+                accw_ref[...] = jnp.zeros_like(accw_ref)
 
     @pl.when(t == 0)
     def _():
@@ -165,7 +171,7 @@
             o_s[pl.ds(pl.multiple_of(r0 + grp * GRP, GRP), GRP), cols] = pick_heads(o2, GRP).astype(BF)
         return carry
 
-    lax.fori_loop(0, NG, self_fwd, 0)
+    lax.fori_loop(0, NG, self_fwd, 0, unroll=True)
 
     attn = dnn(o_s[here, :], wout[0])
     if backward:
@@ -174,7 +180,7 @@
     x1_s[here, :] = x1
 
     qc = dnt(x1, wcq[0]).astype(BF)
-    valid = lax.broadcasted_iota(jnp.int32, (2 * TILE, CAP), 1) < len_ref[s]
+    valid = lax.broadcasted_iota(jnp.int32, (2 * TILE, CAP), 1) < len_ref[s + first]
     for p in range(3):
         cols = slice(p * 128, (p + 1) * 128)
         q2 = stack_heads(qc[:, cols], low, high)
@@ -200,7 +206,7 @@
             m_ref[...] += dnn(hid, wmo[0, cols, :])
             return carry
 
-        lax.fori_loop(0, HID // CH, mlp_fwd, 0)
+        lax.fori_loop(0, HID // CH, mlp_fwd, 0, unroll=True)
         x3 = x2 + mod(5) * m_ref[...]
         for f in range(4):
             for j in range(4):
@@ -232,7 +238,7 @@
         dn_ref[...] += dnt(du, win[0, :, cols])
         return carry
 
-    lax.fori_loop(0, HID // CH, mlp_both, 0)
+    lax.fori_loop(0, HID // CH, mlp_both, 0, unroll=True)
 
     def add_mod(index, value):
         acc_ref[R_MOD + 8 * index:R_MOD + 8 * index + 8, :] += rows8(value)
@@ -279,7 +285,7 @@
             dqkv_s[pl.ds(pl.multiple_of(r0 + grp * GRP, GRP), GRP), 2 * D + p * 128:2 * D + (p + 1) * 128] = dtn(prob.astype(BF), do2).astype(BF)
         return carry
 
-    lax.fori_loop(0, NG, self_bwd, 0)
+    lax.fori_loop(0, NG, self_bwd, 0, unroll=True)
     for j in range(6):
         cols = slice(j * 128, (j + 1) * 128)
         grad = dqk_ref[:, cols]
@@ -322,25 +328,26 @@
         lax.fori_loop(0, 3, mlp_rows, 0)
 
 
-def run_block(index, temporal, backward, x, g, shared):
+def run_block(index, temporal, backward, x, g, shared, first, samples, acc=None):
     mods, msk, cap, lens, weights, tables = shared
-    samples = cap.shape[0]
+    spatial_in = pl.BlockSpec((1, 4, 96, D), lambda s, t: (s + first, t, 0, 0))
     spatial_block = pl.BlockSpec((1, 4, 96, D), lambda s, t: (s, t, 0, 0))
     split_block = pl.BlockSpec((4, 1, 4, 24, D), lambda s, t: (0, s, t, 0, 0))
     cols_block = pl.BlockSpec((4, 1, 12, 8, D), lambda s, t: (0, s, 0, t, 0))
-
-    def const(shape, first=0):
-        return pl.BlockSpec(shape, lambda s, t: (first,) + (0,) * (len(shape) - 1), pipeline_mode=pl.Buffered(1))
-
-    in_specs = [pl.BlockSpec(memory_space=pltpu.SMEM), cols_block if temporal else spatial_block]
+    cols_whole = pl.BlockSpec((4, 1, 12, 8, D), lambda s, t: (0, s + first, 0, t, 0))
+
+    def const(shape, lead=0):
+        return pl.BlockSpec(shape, lambda s, t: (lead,) + (0,) * (len(shape) - 1), pipeline_mode=pl.Buffered(1))
+
+    in_specs = [pl.BlockSpec(memory_space=pltpu.SMEM), cols_block if temporal else spatial_in]
     operands = [lens, x]
     if backward:
-        in_specs.append(cols_block if temporal else split_block)
+        in_specs.append(cols_whole if temporal else split_block)
         operands.append(g)
     in_specs += [
-        pl.BlockSpec((1, 16, D), lambda s, t: (s, 0, 0)),
-        pl.BlockSpec((1, 1, TILE, 1), lambda s, t: (s, t, 0, 0)),
-        pl.BlockSpec((1, CAP, D), lambda s, t: (s, 0, 0)),
+        pl.BlockSpec((1, 16, D), lambda s, t: (s + first, 0, 0)),
+        pl.BlockSpec((1, 1, TILE, 1), lambda s, t: (s + first, t, 0, 0)),
+        pl.BlockSpec((1, CAP, D), lambda s, t: (s + first, 0, 0)),
     ]
     operands += [mods, msk, cap]
     for weight in weights:
@@ -350,6 +357,9 @@
         for table in tables:
             in_specs.append(const(table.shape))
             operands.append(table)
+    if acc is not None:
+        in_specs += [pl.BlockSpec(memory_space=pl.ANY)] * 2
+        operands += list(acc)
 
     def vm(rows, cols, dtype=BF):
         return pltpu.VMEM((rows, cols), dtype)
@@ -379,7 +389,7 @@
         out_specs = split_block
     flops = samples * ROWS * (13 if backward else 4.6) * 1e6
     return pl.pallas_call(
-        functools.partial(block_kernel, temporal, backward),
+        functools.partial(block_kernel, temporal, backward, first, acc is not None),
         grid=(samples, TILES),
         in_specs=in_specs,
         out_specs=out_specs,
@@ -438,10 +448,20 @@
         shared0 = (mods_of(0), msk_rows, cap, caption_len, weights, tables)
         shared1 = (mods_of(1), msk_cols, cap, caption_len, weights, tables)
 
-        middle = run_block(0, False, False, latents, None, shared0)
-        dmid, acc1, accw1 = run_block(1, True, True, exchange(middle), grad_cols, shared1)
-        sum1 = lax.psum((acc1, accw1), ('dp', 'sp'))
-        grad_latents, acc0, accw0 = run_block(0, False, True, latents, exchange(dmid), shared0)
+        cut = samples - 1
+        middle_a = run_block(0, False, False, latents, None, shared0, 0, cut)
+        late, grad_cols = lax.optimization_barrier((latents, grad_cols))
+        middle_b = run_block(0, False, False, late, None, shared0, cut, 1)
+        cols_a = exchange(middle_a)
+        cols_b = exchange(middle_b)
+        dmid_a, *acc1 = run_block(1, True, True, cols_a, grad_cols, shared1, 0, cut)
+        dmid_b, *acc1 = run_block(1, True, True, cols_b, grad_cols, shared1, cut, 1, acc1)
+        back_a = exchange(dmid_a)
+        back_b = exchange(dmid_b)
+        sum1 = lax.psum(tuple(acc1), ('dp', 'sp'))
+        grad_a, *acc0 = run_block(0, False, True, latents, back_a, shared0, 0, cut)
+        grad_b, acc0, accw0 = run_block(0, False, True, latents, back_b, shared0, cut, 1, acc0)
+        grad_latents = jnp.concatenate([grad_a, grad_b], axis=0)
         acc0, accw0, sum1 = lax.optimization_barrier((acc0, accw0, sum1))
         sum0 = lax.psum((acc0, accw0), ('dp', 'sp'))
 

time: 879 us -> 723 us (0.82)
  Pallas kernels: 518 us -> 425 us
  waiting for transfers between devices: 286 us -> 210 us
    pallas_call x3 -> x6, Pallas kernels: 518 us -> 425 us  [run_block(): pl.pallas_call(functools.partial(block_kernel, temporal, backward, first,...]
    all_to_all x2 -> x4, waiting for transfers between devices: 75.3 us -> 0.01 us  [the longest x1 0.01 us: local_step(): cols_a = exchange(middle_a)]
    all_to_all x1, waiting for transfers between devices: 25.8 us -> 0.01 us  [local_step(): grad_cols = exchange(grad_split)]
    psum x1, waiting for transfers between devices: 0.02 us -> 20.6 us  [local_step(): sum1 = lax.psum(tuple(acc1), ('dp', 'sp'))]
  transfers between devices with their start and end apart: 5 -> 7, of which waited for: 4 -> 2; matrix products, arithmetic and copies ran while one was open for 2% -> 2% of each run, Pallas kernels for 23% -> 59%
where the time goes in v2:
time: 723 us; the launch traced here: 717 us
  Pallas kernels  425 us (59%)
  waiting for transfers between devices  210 us (29%)
  local copies, waits for them, and re-layouts  28.9 us (4%)
  starting transfers between devices  21.9 us (3%)
  other arithmetic  16.3 us (2%)
  between operations  14.8 us (2%)
    pallas_call x6, Pallas kernels, run_block(): pl.pallas_call(functools.partial(block_kernel, temporal, backward, first,...  425 us
    psum x1, waiting for transfers between devices, local_step(): sum0 = lax.psum((acc0, accw0), ('dp', 'sp'))  189 us
    psum x1, waiting for transfers between devices, local_step(): sum1 = lax.psum(tuple(acc1), ('dp', 'sp'))  20.6 us
  transfers between devices with their start and end apart: 7, of which 2 were waited for; matrix products, arithmetic and copies ran while one was open for 2% of the time, Pallas kernels for 59%

profile of v2, /device:TPU:0, one launch (start us, length us, event | category | flops | bytes accessed | tf_op | source)
XLA Modules:
  0.0 716.5 jit_solution(2642951785684856583)
XLA Ops:
  7.2 3.5 copy.56
  10.7 4.7 all-to-all-start.1
  15.6 2.9 reshape_reshape.4.refs_2_.refs_3_
  20.0 37.7 %spatial_fwd.2 = bf16[4,2,12,24,384]{4,3,2,1,0:T(8,128)(2,1)} custom-call(s32[3]{0:T(128)} %len_ref.11, bf16[3,12,96,384]{3,2,1,0:T(8,128)(2,1)} %refs_0_.6, f32[3,16,384]{2,1,0:T(8,128)} %select_maximum_fusion.1.refs_1_.refs_2_, f32[3,3,384,1]{3,2,1,0:T(8,128)} %reshape_reshape.4.refs_2_.refs_3_, bf16[3,128,384]{2,1,0:T(8,128)(2,1)} %pad.19.refs_3_.refs_4_, ...), custom_call_target="tpu_custom_call" | custom-call | flops 10598400000 | bytes 20000000 | tf_op jit(solution)/shard_map/spatial_fwd/pallas_call | solution.py:391
  57.8 4.9 all-to-all-start
  64.7 2.1 tile.36.refs_3_
  68.3 20.5 %spatial_fwd.3 = bf16[4,1,12,24,384]{4,3,2,1,0:T(8,128)(2,1)} custom-call(s32[3]{0:T(128)} %len_ref.11, bf16[3,12,96,384]{3,2,1,0:T(8,128)(2,1)} %refs_0_.6, f32[3,16,384]{2,1,0:T(8,128)} %select_maximum_fusion.1.refs_1_.refs_2_, f32[3,3,384,1]{3,2,1,0:T(8,128)} %reshape_reshape.4.refs_2_.refs_3_, bf16[3,128,384]{2,1,0:T(8,128)(2,1)} %pad.19.refs_3_.refs_4_, ...), custom_call_target="tpu_custom_call" | custom-call | flops 5299200000 | bytes 20000000 | tf_op jit(solution)/shard_map/spatial_fwd/pallas_call | solution.py:391
  88.8 4.3 all-to-all-start.3
  93.1 123.3 %temporal_bwd.2 = (bf16[4,2,12,24,384]{4,3,2,1,0:T(8,128)(2,1)}, f32[4656,384]{1,0:T(8,128)}, f32[384,1536]{1,0:T(8,128)}) custom-call(s32[3]{0:T(128)} %len_ref.11, bf16[4,2,12,24,384]{4,3,2,1,0:T(8,128)(2,1)} %all-to-all-done.refs_0_, bf16[4,3,12,24,384]{4,3,2,1,0:T(8,128)(2,1)} %all-to-all-done.1.refs_1_, f32[3,16,384]{2,1,0:T(8,128)} %select_maximum_fusion.refs_2_, ...), custom_call_target="tpu_custom_call" | custom-call | flops 29952000000 | bytes 20000000 | tf_op jit(solution)/shard_map/temporal_bwd/pallas_call | solution.py:391
  216.4 4.4 all-to-all-start.2
  220.8 69.3 %temporal_bwd.3 = (bf16[4,1,12,24,384]{4,3,2,1,0:T(8,128)(2,1)}, f32[4656,384]{1,0:T(8,128)}, f32[384,1536]{1,0:T(8,128)}) custom-call(s32[3]{0:T(128)} %len_ref.11, bf16[4,1,12,24,384]{4,3,2,1,0:T(8,128)(2,1)} %copy-done.8, bf16[4,3,12,24,384]{4,3,2,1,0:T(8,128)(2,1)} %all-to-all-done.1.refs_1_, f32[3,16,384]{2,1,0:T(8,128)} %select_maximum_fusion.refs_2_, ...), custom_call_target="tpu_custom_call" | custom-call | flops 14976000000 | bytes 20000000 | tf_op jit(solution)/shard_map/temporal_bwd/pallas_call | solution.py:391
  290.2 3.5 all-to-all-start.4
  293.7 110.8 %spatial_bwd.2 = (bf16[2,12,96,384]{3,2,1,0:T(8,128)(2,1)}, f32[4656,384]{1,0:T(8,128)}, f32[384,1536]{1,0:T(8,128)}) custom-call(s32[3]{0:T(128)} %len_ref.11, bf16[3,12,96,384]{3,2,1,0:T(8,128)(2,1)} %refs_0_.6, bf16[4,2,12,24,384]{4,3,2,1,0:T(8,128)(2,1)} %all-to-all-done.2.refs_1_, f32[3,16,384]{2,1,0:T(8,128)} %select_maximum_fusion.1.refs_1_.refs_2_, ...), custom_call_target="tpu_custom_call" | custom-call | flops 29952000000 | bytes 20000000 | tf_op jit(solution)/shard_map/spatial_bwd/pallas_call | solution.py:391
  405.5 63.1 %spatial_bwd.3 = (bf16[1,12,96,384]{3,2,1,0:T(8,128)(2,1)}, f32[4656,384]{1,0:T(8,128)}, f32[384,1536]{1,0:T(8,128)}) custom-call(s32[3]{0:T(128)} %len_ref.11, bf16[3,12,96,384]{3,2,1,0:T(8,128)(2,1)} %refs_0_.6, bf16[4,1,12,24,384]{4,3,2,1,0:T(8,128)(2,1)} %copy-done.9, f32[3,16,384]{2,1,0:T(8,128)} %select_maximum_fusion.1.refs_1_.refs_2_, ...), custom_call_target="tpu_custom_call" | custom-call | flops 14976000000 | bytes 20000000 | tf_op jit(solution)/shard_map/spatial_bwd/pallas_call | solution.py:391
  468.6 20.6 %all-reduce.12.cloned.1.call-done = (f32[4656,384]{1,0:T(8,128)}, f32[384,1536]{1,0:T(8,128)}) async-done(((f32[4656,384]{1,0:T(8,128)}, f32[384,1536]{1,0:T(8,128)}), (f32[4656,384]{1,0:T(8,128)}, f32[384,1536]{1,0:T(8,128)})) %all-reduce.12.cloned.1.call-update) | async-done | bytes 9510928 | tf_op jit(solution)/shard_map/psum | solution.py:461
  489.2 1.4 copy-done.7
  490.9 1.8 pad_maximum_fusion.2
  492.7 2.1 slice.59
  495.2 1.3 slice.53
  497.2 1.2 fusion.10
  498.6 189.3 %all-reduce.10.cloned.1.call-done = (f32[4656,384]{1,0:T(8,128)}, f32[1,384,1536]{2,1,0:T(8,128)}) async-done(((f32[4656,384]{1,0:T(8,128)}, f32[1,384,1536]{2,1,0:T(8,128)}), (f32[4656,384]{1,0:T(8,128)}, f32[1,384,1536]{2,1,0:T(8,128)})) %all-reduce.10.cloned.1.call-update) | async-done | bytes 9510928 | tf_op jit(solution)/shard_map/psum | solution.py:466
  688.7 1.3 slice.69
  690.1 1.6 slice.66
  691.7 1.6 fusion.9
  693.3 2.0 slice_bitcast_fusion
  696.4 2.5 pad_maximum_fusion
  698.9 1.6 maximum_bitcast_fusion.1
  701.2 2.2 maximum_bitcast_fusion
  703.3 2.5 pad_maximum_fusion.1
  705.8 1.1 pad_maximum_fusion.4
  707.1 1.1 maximum_bitcast_fusion.2
  708.2 1.1 pad_maximum_fusion.3
  (67 shorter events, 10.3 us)
Async XLA Ops:
  10.7 4.7 copy-start.16
  10.7 7.8 %copy-start.12 = (bf16[3,120,384]{2,1,0:T(8,128)(2,1)S(1)}, bf16[3,120,384]{2,1,0:T(8,128)(2,1)}, u32[]{:S(2)}) copy-start(bf16[3,120,384]{2,1,0:T(8,128)(2,1)} %param.19) | copy-start | bytes 829444
  10.7 47.1 %all-to-all-start.1 = ((bf16[4,3,12,24,384]{4,3,2,1,0:T(8,128)(2,1)}), bf16[4,3,12,24,384]{4,3,2,1,0:T(8,128)(2,1)}, u32[]{:S(2)}, u32[]{:S(2)}) async-start(bf16[4,3,12,24,384]{4,3,2,1,0:T(8,128)(2,1)} %bitcast.46), calls=%async_computation.1 | async-start | bytes 5308416 | tf_op jit(solution)/shard_map/all_to_all | solution.py:427
  15.4 3.9 copy-start.15
  15.4 3.9 copy-start.13
  15.4 3.9 copy-start.14
  57.8 31.0 %all-to-all-start = ((bf16[4,2,12,24,384]{4,3,2,1,0:T(8,128)(2,1)}), bf16[4,2,12,24,384]{4,3,2,1,0:T(8,128)(2,1)}, u32[]{:S(2)}, u32[]{:S(2)}) async-start(bf16[4,2,12,24,384]{4,3,2,1,0:T(8,128)(2,1)} %spatial_fwd.2), calls=%async_computation | async-start | bytes 3538944 | tf_op jit(solution)/shard_map/all_to_all | solution.py:455
  88.8 127.6 %all-to-all-start.3 = ((bf16[4,1,12,24,384]{4,3,2,1,0:T(8,128)(2,1)}), bf16[4,1,12,24,384]{4,3,2,1,0:T(8,128)(2,1)S(1)}, u32[]{:S(2)}, u32[]{:S(2)}) async-start(bf16[4,1,12,24,384]{4,3,2,1,0:T(8,128)(2,1)} %spatial_fwd.3), calls=%async_computation.3 | async-start | bytes 1769472 | tf_op jit(solution)/shard_map/all_to_all | solution.py:456
  216.4 4.5 copy-start.8
  216.4 73.8 %all-to-all-start.2 = ((bf16[4,2,12,24,384]{4,3,2,1,0:T(8,128)(2,1)}), bf16[4,2,12,24,384]{4,3,2,1,0:T(8,128)(2,1)}, u32[]{:S(2)}, u32[]{:S(2)}) async-start(bf16[4,2,12,24,384]{4,3,2,1,0:T(8,128)(2,1)} %get-tuple-element.28), calls=%async_computation.2 | async-start | bytes 3538944 | tf_op jit(solution)/shard_map/all_to_all | solution.py:459
  220.8 268.4 %all-reduce.12.cloned.1.call-start = ((), (), s32[]{:S(2)}) async-start(), calls=%async_computation.6 | async-start | bytes 19021824 | tf_op jit(solution)/shard_map/psum | solution.py:461
  290.2 114.4 %all-to-all-start.4 = ((bf16[4,1,12,24,384]{4,3,2,1,0:T(8,128)(2,1)}), bf16[4,1,12,24,384]{4,3,2,1,0:T(8,128)(2,1)S(1)}, u32[]{:S(2)}, u32[]{:S(2)}) async-start(bf16[4,1,12,24,384]{4,3,2,1,0:T(8,128)(2,1)} %get-tuple-element.33), calls=%async_computation.4 | async-start | bytes 1769472 | tf_op jit(solution)/shard_map/all_to_all | solution.py:460
  293.7 394.2 %all-reduce.10.cloned.1.call-start = ((), (), s32[]{:S(2)}) async-start(), calls=%async_computation.5 | async-start | bytes 19021824 | tf_op jit(solution)/shard_map/psum | solution.py:466
  404.6 0.9 copy-start.9
  489.2 1.5 copy-start.7
  489.2 1.7 copy-start.10
  490.9 4.3 copy-start
  691.7 3.6 copy-start.11
  693.3 2.7 copy-start.5
  693.3 3.1 copy-start.6
  698.9 2.3 copy-start.1
  703.3 2.5 copy-start.4
  705.8 1.2 copy-start.3
  705.8 2.3 copy-start.2
Sparse Core Ops, SparseCore 0:
  290.3 198.8 all-reduce.11
  495.7 192.0 all-reduce.9
